TPU v7x, 256 devices: a whole 4x4x8 slice. The times are simulated.
256 devices in a mesh: space: 4 (over z_hi, core), fsdp: 64 (over y, x, z_lo).
Axes of the slice: x: 4, y: 4, z: 8 (z_hi: 2, z_lo: 4; z = z_hi * 4 + z_lo), core: 2. Of those that a mesh axis runs over, the one named last changes fastest.
Arguments:
- acts: bfloat16 [64, 8, 16, 16, 512], P('fsdp', 'space'), may hold values from -16 to 16
- kernel: bfloat16 [512, 27, 256], P('fsdp'), may hold values from -0.0546875 to 0.0546875
- cotangent: bfloat16 [64, 8, 16, 16, 256], P('fsdp', 'space'), may hold values from -6 to 6
Outputs:
- outputs: bfloat16 [64, 8, 16, 16, 256], P('fsdp', 'space')
- grad_input: bfloat16 [64, 8, 16, 16, 512], P('fsdp', 'space')
- grad_kernel: float32 [512, 27, 256], P('fsdp')
All inputs are finite; a program needn't handle non-finite values.
Results may differ from a plain program's by a relative error of at most 0.0095.
Values may be sent and summed in bfloat16 or wider, within the bound.
A program may use at most 128 MiB of HBM per device.

v0:
```python
import jax
import jax.numpy as jnp
from jax import lax
from jax.sharding import PartitionSpec as P

kernel_offsets = [(i // 9 - 1, i // 3 % 3 - 1, i % 3 - 1) for i in range(27)]


def padded(block, sides, width):
    for axis, dim in sides:
        count = lax.axis_size(axis)
        forward = [(i, i + 1) for i in range(count - 1)]
        backward = [(target, source) for source, target in forward]
        low = lax.ppermute(
            lax.slice_in_dim(block, block.shape[dim] - width, None, axis=dim), axis, forward
        )
        high = lax.ppermute(lax.slice_in_dim(block, 0, width, axis=dim), axis, backward)
        block = jnp.concatenate([low, block, high], axis=dim)
    return block


def from_everyone(x, axis):
    copies = jnp.broadcast_to(x, (lax.axis_size(axis), *x.shape))
    return lax.all_to_all(copies, axis, split_axis=0, concat_axis=0, tiled=True)


def of_everyone(x, axis):
    everything = from_everyone(x, axis)
    return jnp.sum(everything.astype(jnp.float32), axis=0)


def body(acts, kernel, cotangent):
    local_acts = acts[0]
    local_grad = cotangent[0]
    slab_len = local_acts.shape[0]
    side_len = local_acts.shape[1]
    chan_in = local_acts.shape[3]
    chan_out = local_grad.shape[3]
    tap_count = len(kernel_offsets)
    padded_side = side_len + 2
    plane = padded_side * padded_side
    margin = padded_side + 1
    grid_rows = slab_len * plane
    centre = margin + plane
    acts_float = local_acts.astype(jnp.float32)
    squash = jax.nn.sigmoid(acts_float)
    hidden = (acts_float * squash).astype(jnp.bfloat16)
    joined = jnp.concatenate([hidden, local_grad], axis=3)[None]
    framed = padded(joined, (("space", 1),), 1)[0]
    framed = jnp.pad(framed, ((0, 0), (1, 1), (1, 1), (0, 0)))
    flat_all = framed.reshape((slab_len + 2) * plane, chan_in + chan_out)
    flat_all = jnp.pad(flat_all, ((margin, margin), (0, 0)))
    hidden_flat = flat_all[:, :chan_in]
    grad_flat_pad = flat_all[:, chan_in:]
    grad_centre = grad_flat_pad[centre : centre + grid_rows]

    def offset_of(tap_index):
        shift_d, shift_h, shift_w = kernel_offsets[tap_index]
        return shift_d * plane + shift_h * padded_side + shift_w

    empty_out = jnp.zeros((grid_rows, chan_out), jnp.float32)
    running = empty_out
    shard_rows = lax.all_gather(kernel, "fsdp", axis=0, tiled=True)
    channel_part = hidden_flat
    for tap_index in range(tap_count):
        begin = centre + offset_of(tap_index)
        running = running + jnp.dot(
            channel_part[begin : begin + grid_rows],
            shard_rows[:, tap_index, :],
            preferred_element_type=jnp.float32,
        )
    shard_rows = lax.all_gather(kernel, "fsdp", axis=0, tiled=True)
    row_count = shard_rows.shape[0]
    total = jnp.zeros((grid_rows, row_count), jnp.float32)
    for tap_index in range(tap_count):
        begin = centre - offset_of(tap_index)
        total = total + lax.dot_general(
            grad_flat_pad[begin : begin + grid_rows],
            shard_rows[:, tap_index, :],
            (((1,), (1,)), ((), ())),
            preferred_element_type=jnp.float32,
        )
    back = total.reshape(1, slab_len, padded_side, padded_side, row_count)
    back_inner = back[0][:, 1:-1, 1:-1, :]
    grad_input = (back_inner * squash * (1.0 + acts_float * (1.0 - squash))).astype(jnp.bfloat16)[
        None
    ]
    batch_scale = 1.0 / lax.axis_size("fsdp")
    channel_part = hidden_flat
    pieces = []
    for tap_index in range(tap_count):
        begin = centre + offset_of(tap_index)
        pieces.append(
            lax.dot_general(
                channel_part[begin : begin + grid_rows],
                grad_centre,
                (((0,), (0,)), ((), ())),
                preferred_element_type=jnp.float32,
            )
        )
    term = jnp.concatenate(pieces, axis=1)
    owned_share = lax.psum_scatter(
        term.reshape(kernel.shape[0] * lax.axis_size("fsdp"), tap_count, chan_out) * batch_scale,
        "fsdp",
        scatter_dimension=0,
        tiled=True,
    )
    grad_kernel = of_everyone(owned_share.astype(jnp.bfloat16), "space").astype(jnp.float32)
    shaped = running.reshape(slab_len, padded_side, padded_side, running.shape[-1])
    outputs = shaped[:, 1:-1, 1:-1, :].astype(jnp.bfloat16)[None]
    return (outputs, grad_input, grad_kernel)


def solution(mesh):
    return jax.shard_map(
        body,
        mesh=mesh,
        in_specs=(
            P("fsdp", "space", None, None, None),
            P("fsdp", None, None),
            P("fsdp", "space", None, None, None),
        ),
        out_specs=(
            P("fsdp", "space", None, None, None),
            P("fsdp", "space", None, None, None),
            P("fsdp", None, None),
        ),
        check_vma=False,
    )
```

profile of v0, /device:TPU:1, one launch (start us, length us, event | category | flops | bytes accessed | tf_op | source)
XLA Modules:
  0.0 806.9 jit_solution(10638212462257670923)
XLA Ops:
  7.9 1.4 fusion.4
  10.4 10.2 %collective-permute-start = (bf16[1,1,16,16,768]{4,3,2,1,0:T(8,128)(2,1)S(1)}, bf16[1,1,16,16,768]{4,3,2,1,0:T(8,128)(2,1)S(1)}, u32[]{:S(2)}, u32[]{:S(2)}) collective-permute-start(bf16[1,1,16,16,768]{4,3,2,1,0:T(8,128)(2,1)S(1)} %get-tuple-element.3), channel_id=1, source_target_pairs={{0,64},{64,128},{128,192},{1,65},{65,129},{129,193},{2,66},{66,130... | collective-permute-start | bytes 1179656 | tf_op jit(solution)/shard_map/ppermute | solution.py:14
  20.6 1.9 collective-permute-start.1
  22.5 3.6 collective-permute-done
  26.1 13.8 %collective-permute-done.1 = bf16[1,1,16,16,768]{4,3,2,1,0:T(8,128)(2,1)S(1)} collective-permute-done((bf16[1,1,16,16,768]{4,3,2,1,0:T(8,128)(2,1)S(1)}, bf16[1,1,16,16,768]{4,3,2,1,0:T(8,128)(2,1)S(1)}, u32[]{:S(2)}, u32[]{:S(2)}) %collective-permute-start.1) | collective-permute-done | bytes 393248 | tf_op jit(solution)/shard_map/ppermute | solution.py:17
  40.0 2.6 pad.8
  42.7 2.9 reshape.18
  64.3 1.3 convolution_dynamic-update-slice_fusion.11
  65.6 1.3 convolution_dynamic-update-slice_fusion.10
  66.9 1.3 convolution_dynamic-update-slice_fusion.9
  79.4 12.1 %broadcast_multiply_fusion = f32[512,6912]{0,1:T(8,128)} fusion(f32[512,6912]{0,1:T(8,128)} %convolution_dynamic-update-slice_fusion), kind=kLoop, calls=%fused_computation | loop fusion | flops 3538944 | bytes 28311552 | tf_op jit(solution)/shard_map/mul | solution.py:103
  91.5 19.9 %copy.10 = f32[512,27,256]{2,1,0:T(8,128)} copy(f32[512,27,256]{0,2,1:T(8,128)} %bitcast.124) | data formatting | bytes 28311552 | tf_op jit(solution)/shard_map/mul | solution.py:103
  111.5 195.9 %all-gather.2.cloned.1.call-done = bf16[512,27,256]{2,0,1:T(8,128)(2,1)} async-done(((bf16[8,27,256]{2,0,1:T(8,128)(2,1)}), bf16[512,27,256]{2,0,1:T(8,128)(2,1)}) %all-gather.2.cloned.1.call-update) | async-done | bytes 7077904 | tf_op jit(solution)/shard_map/all_gather | solution.py:63
  307.4 1.3 fusion.61
  308.7 1.5 fusion.89
  310.2 1.7 convolution_add_fusion.51
  331.7 401.0 %reduce-scatter.2.cloned.1.call-done = f32[8,27,256]{2,1,0:T(8,128)} async-done(((f32[512,27,256]{2,1,0:T(8,128)}), f32[8,27,256]{2,1,0:T(8,128)}) %reduce-scatter.2.cloned.1.call-update) | async-done | bytes 221200 | tf_op jit(solution)/shard_map/reduce_scatter | solution.py:102
  734.5 52.8 %all-to-all-start = ((bf16[4,8,27,256]{3,1,2,0:T(8,128)(2,1)}), bf16[4,8,27,256]{3,1,2,0:T(8,128)(2,1)}, u32[]{:S(2)}, u32[]{:S(2)}) async-start(bf16[4,8,27,256]{3,1,2,0:T(8,128)(2,1)} %broadcast_in_dim.15), calls=%async_computation.1 | async-start | bytes 884736 | tf_op jit(solution)/shard_map/all_to_all | solution.py:24
  787.3 2.2 fusion
  789.6 1.8 reshape.19
  791.6 1.8 slice_bitcast_fusion
  793.4 2.3 fusion.63
  795.7 2.6 all-to-all-done
  798.3 1.8 convert_reduce_fusion
  (86 shorter events, 53.4 us)
Async XLA Ops:
  7.2 300.3 %all-gather.2.cloned.1.call-start = ((), (), s32[]{:S(2)}) async-start(), calls=%async_computation.2 | async-start | bytes 7188480 | tf_op jit(solution)/shard_map/all_gather | solution.py:63
  7.9 724.8 %reduce-scatter.2.cloned.1.call-start = ((), (), s32[]{:S(2)}) async-start(), calls=%async_computation.3 | async-start | bytes 17039360 | tf_op jit(solution)/shard_map/reduce_scatter | solution.py:102
  10.4 15.7 %collective-permute-start = (bf16[1,1,16,16,768]{4,3,2,1,0:T(8,128)(2,1)S(1)}, bf16[1,1,16,16,768]{4,3,2,1,0:T(8,128)(2,1)S(1)}, u32[]{:S(2)}, u32[]{:S(2)}) collective-permute-start(bf16[1,1,16,16,768]{4,3,2,1,0:T(8,128)(2,1)S(1)} %get-tuple-element.3), channel_id=1, source_target_pairs={{0,64},{64,128},{128,192},{1,65},{65,129},{129,193},{2,66},{66,130... | collective-permute-start | bytes 1179656 | tf_op jit(solution)/shard_map/ppermute | solution.py:14
  20.6 19.3 %collective-permute-start.1 = (bf16[1,1,16,16,768]{4,3,2,1,0:T(8,128)(2,1)S(1)}, bf16[1,1,16,16,768]{4,3,2,1,0:T(8,128)(2,1)S(1)}, u32[]{:S(2)}, u32[]{:S(2)}) collective-permute-start(bf16[1,1,16,16,768]{4,3,2,1,0:T(8,128)(2,1)S(1)} %get-tuple-element.4), channel_id=1, source_target_pairs={{64,0},{128,64},{192,128},{65,1},{129,65},{193,129},{66,2},{130,66... | collective-permute-start | bytes 1179656 | tf_op jit(solution)/shard_map/ppermute | solution.py:17
  308.7 3.2 copy-start
  734.5 63.8 %all-to-all-start = ((bf16[4,8,27,256]{3,1,2,0:T(8,128)(2,1)}), bf16[4,8,27,256]{3,1,2,0:T(8,128)(2,1)}, u32[]{:S(2)}, u32[]{:S(2)}) async-start(bf16[4,8,27,256]{3,1,2,0:T(8,128)(2,1)} %broadcast_in_dim.15), calls=%async_computation.1 | async-start | bytes 884736 | tf_op jit(solution)/shard_map/all_to_all | solution.py:24
Sparse Core Ops, SparseCore 0:
  9.7 297.7 all-gather.1
  310.0 422.6 reduce-scatter.1
where the time goes:
time: 808 us; the launch traced here: 807 us
  waiting for transfers between devices  618 us (76%)
  starting transfers between devices  65 us (8%)
  matrix products  59.8 us (7%)
  local copies, waits for them, and re-layouts  31.2 us (4%)
  other arithmetic  18.7 us (2%)
  between operations  14.5 us (2%)
    reduce_scatter x1, waiting for transfers between devices, body(): lax.psum_scatter(term.reshape(kernel.shape[0] * lax.axis_size('fsdp'), ta...  401 us
    all_gather x1, waiting for transfers between devices, body(): shard_rows = lax.all_gather(kernel, 'fsdp', axis=0, tiled=True)  196 us
    all_to_all x1, starting transfers between devices, from_everyone(): return lax.all_to_all(copies, axis, split_axis=0, concat_axis=0, tiled=True)  52.8 us
    dot_general x27, matrix products, body(): lax.dot_general(channel_part[begin:begin + grid_rows], grad_centre, (((0,...  33.8 us
    mul x1, local copies, waits for them, and re-layouts, body(): term.reshape(kernel.shape[0] * lax.axis_size('fsdp'), tap_count, chan_out)  19.9 us
  transfers between devices with their start and end apart: 5, of which 5 were waited for; matrix products, arithmetic and copies ran while one was open for 13% of the time, Pallas kernels for 0%

commit v1 on v0

--- a/solution.py
+++ b/solution.py
@@ -60,7 +60,9 @@
 
     empty_out = jnp.zeros((grid_rows, chan_out), jnp.float32)
     running = empty_out
-    shard_rows = lax.all_gather(kernel, "fsdp", axis=0, tiled=True)
+    shard_rows = jnp.concatenate(
+        lax.all_to_all(jnp.stack([kernel] * lax.axis_size("fsdp")), "fsdp", 0, 0), axis=0
+    )
     channel_part = hidden_flat
     for tap_index in range(tap_count):
         begin = centre + offset_of(tap_index)

time: 808 us -> 882 us (1.092)
  waiting for transfers between devices: 618 us -> 666 us
  other arithmetic: 18.7 us -> 28.1 us
    all_to_all x0 -> x1, waiting for transfers between devices: none -> 150 us  [body(): lax.all_to_all(jnp.stack([kernel] * lax.axis_size('fsdp')), 'fsdp', 0, 0)]
    all_gather x1, waiting for transfers between devices: 196 us -> 96.4 us  [body(): shard_rows = lax.all_gather(kernel, 'fsdp', axis=0, tiled=True)]
    mul x1, other arithmetic: 12.1 us -> 21.4 us  [body(): term.reshape(kernel.shape[0] * lax.axis_size('fsdp'), tap_count, chan_out)]
    all_to_all x0 -> x1, starting transfers between devices: none -> 9.26 us  [body(): lax.all_to_all(jnp.stack([kernel] * lax.axis_size('fsdp')), 'fsdp', 0, 0)]
  transfers between devices with their start and end apart: 5 -> 6, of which waited for: 5 -> 5; matrix products, arithmetic and copies ran while one was open for 13% -> 14% of each run, Pallas kernels for 0% -> 0%
where the time goes in v1:
time: 882 us; the launch traced here: 877 us
  waiting for transfers between devices  666 us (76%)
  starting transfers between devices  72.8 us (8%)
  matrix products  59 us (7%)
  local copies, waits for them, and re-layouts  36.9 us (4%)
  other arithmetic  28.1 us (3%)
  between operations  14.8 us (2%)
    reduce_scatter x1, waiting for transfers between devices, body(): lax.psum_scatter(term.reshape(kernel.shape[0] * lax.axis_size('fsdp'), ta...  406 us
    all_to_all x1, waiting for transfers between devices, body(): lax.all_to_all(jnp.stack([kernel] * lax.axis_size('fsdp')), 'fsdp', 0, 0)  150 us
    all_gather x1, waiting for transfers between devices, body(): shard_rows = lax.all_gather(kernel, 'fsdp', axis=0, tiled=True)  96.4 us
    all_to_all x1, starting transfers between devices, from_everyone(): return lax.all_to_all(copies, axis, split_axis=0, concat_axis=0, tiled=True)  51.3 us
    dot_general x27, matrix products, body(): lax.dot_general(channel_part[begin:begin + grid_rows], grad_centre, (((0,...  34 us
    mul x1, other arithmetic, body(): term.reshape(kernel.shape[0] * lax.axis_size('fsdp'), tap_count, chan_out)  21.4 us
    mul x1, local copies, waits for them, and re-layouts, body(): term.reshape(kernel.shape[0] * lax.axis_size('fsdp'), tap_count, chan_out)  19.9 us
  transfers between devices with their start and end apart: 6, of which 5 were waited for; matrix products, arithmetic and copies ran while one was open for 14% of the time, Pallas kernels for 0%

profile of v1, /device:TPU:1, one launch (start us, length us, event | category | flops | bytes accessed | tf_op | source)
XLA Modules:
  0.0 877.2 jit_solution(11566188731762582819)
XLA Ops:
  7.9 1.4 fusion.4
  10.4 10.2 %collective-permute-start = (bf16[1,1,16,16,768]{4,3,2,1,0:T(8,128)(2,1)S(1)}, bf16[1,1,16,16,768]{4,3,2,1,0:T(8,128)(2,1)S(1)}, u32[]{:S(2)}, u32[]{:S(2)}) collective-permute-start(bf16[1,1,16,16,768]{4,3,2,1,0:T(8,128)(2,1)S(1)} %get-tuple-element.3), channel_id=1, source_target_pairs={{0,64},{64,128},{128,192},{1,65},{65,129},{129,193},{2,66},{66,130... | collective-permute-start | bytes 1179656 | tf_op jit(solution)/shard_map/ppermute | solution.py:14
  20.6 1.9 collective-permute-start.1
  22.5 3.4 stack.2
  25.9 9.3 %all-to-all-start = ((bf16[64,8,27,256]{3,1,2,0:T(8,128)(2,1)}), bf16[64,8,27,256]{3,1,2,0:T(8,128)(2,1)}, u32[]{:S(2)}, u32[]{:S(2)}) async-start(bf16[64,8,27,256]{3,1,2,0:T(8,128)(2,1)} %stack.2), calls=%async_computation | async-start | bytes 14155776 | tf_op jit(solution)/shard_map/all_to_all | solution.py:64
  35.2 7.4 collective-permute-done.1
  42.8 2.6 pad.8
  45.5 3.1 reshape.23
  67.4 1.3 convolution_dynamic-update-slice_fusion.11
  68.7 1.3 convolution_dynamic-update-slice_fusion.10
  70.0 1.3 convolution_dynamic-update-slice_fusion.9
  82.6 21.4 %broadcast_multiply_fusion = f32[512,6912]{0,1:T(8,128)} fusion(f32[512,6912]{0,1:T(8,128)} %convolution_dynamic-update-slice_fusion), kind=kLoop, calls=%fused_computation.1 | loop fusion | flops 3538944 | bytes 28311552 | tf_op jit(solution)/shard_map/mul | solution.py:105
  104.0 19.9 %copy.13 = f32[512,27,256]{2,1,0:T(8,128)} copy(f32[512,27,256]{0,2,1:T(8,128)} %bitcast.181) | data formatting | bytes 28311552 | tf_op jit(solution)/shard_map/mul | solution.py:105
  123.9 150.5 %all-to-all-done = bf16[64,8,27,256]{3,1,2,0:T(8,128)(2,1)} async-done(((bf16[64,8,27,256]{3,1,2,0:T(8,128)(2,1)}), bf16[64,8,27,256]{3,1,2,0:T(8,128)(2,1)}, u32[]{:S(2)}, u32[]{:S(2)}) %all-to-all-start) | async-done | bytes 7077920 | tf_op jit(solution)/shard_map/all_to_all | solution.py:64
  274.4 3.9 copy.18
  288.4 96.4 %all-gather.2.cloned.1.call-done = bf16[512,27,256]{2,0,1:T(8,128)(2,1)} async-done(((bf16[8,27,256]{2,0,1:T(8,128)(2,1)}), bf16[512,27,256]{2,0,1:T(8,128)(2,1)}) %all-gather.2.cloned.1.call-update) | async-done | bytes 7077904 | tf_op jit(solution)/shard_map/all_gather | solution.py:74
  384.9 1.5 fusion.89
  386.3 1.7 convolution_add_fusion.25
  397.9 406.2 %reduce-scatter.2.cloned.1.call-done = f32[8,27,256]{2,1,0:T(8,128)} async-done(((f32[512,27,256]{2,1,0:T(8,128)}), f32[8,27,256]{2,1,0:T(8,128)}) %reduce-scatter.2.cloned.1.call-update) | async-done | bytes 221200 | tf_op jit(solution)/shard_map/reduce_scatter | solution.py:104
  806.0 51.3 %all-to-all-start.1 = ((bf16[4,8,27,256]{3,1,2,0:T(8,128)(2,1)}), bf16[4,8,27,256]{3,1,2,0:T(8,128)(2,1)}, u32[]{:S(2)}, u32[]{:S(2)}) async-start(bf16[4,8,27,256]{3,1,2,0:T(8,128)(2,1)} %broadcast_in_dim.15), calls=%async_computation.2 | async-start | bytes 884736 | tf_op jit(solution)/shard_map/all_to_all | solution.py:24
  857.3 2.3 fusion
  861.6 2.3 fusion.63
  863.9 4.4 all-to-all-done.1
  868.3 1.8 convert_reduce_fusion
  (94 shorter events, 55.6 us)
Async XLA Ops:
  7.2 377.7 %all-gather.2.cloned.1.call-start = ((), (), s32[]{:S(2)}) async-start(), calls=%async_computation.3 | async-start | bytes 7188480 | tf_op jit(solution)/shard_map/all_gather | solution.py:74
  7.9 14.6 %copy-start.2 = (bf16[8,27,256]{2,0,1:T(8,128)(2,1)S(1)}, bf16[8,27,256]{2,0,1:T(8,128)(2,1)}, u32[]{:S(2)}) copy-start(bf16[8,27,256]{2,0,1:T(8,128)(2,1)} %param.4) | copy-start | bytes 331780
  10.4 24.8 %collective-permute-start = (bf16[1,1,16,16,768]{4,3,2,1,0:T(8,128)(2,1)S(1)}, bf16[1,1,16,16,768]{4,3,2,1,0:T(8,128)(2,1)S(1)}, u32[]{:S(2)}, u32[]{:S(2)}) collective-permute-start(bf16[1,1,16,16,768]{4,3,2,1,0:T(8,128)(2,1)S(1)} %get-tuple-element.3), channel_id=1, source_target_pairs={{0,64},{64,128},{128,192},{1,65},{65,129},{129,193},{2,66},{66,130... | collective-permute-start | bytes 1179656 | tf_op jit(solution)/shard_map/ppermute | solution.py:14
  20.6 22.1 %collective-permute-start.1 = (bf16[1,1,16,16,768]{4,3,2,1,0:T(8,128)(2,1)S(1)}, bf16[1,1,16,16,768]{4,3,2,1,0:T(8,128)(2,1)S(1)}, u32[]{:S(2)}, u32[]{:S(2)}) collective-permute-start(bf16[1,1,16,16,768]{4,3,2,1,0:T(8,128)(2,1)S(1)} %get-tuple-element.4), channel_id=1, source_target_pairs={{64,0},{128,64},{192,128},{65,1},{129,65},{193,129},{66,2},{130,66... | collective-permute-start | bytes 1179656 | tf_op jit(solution)/shard_map/ppermute | solution.py:17
  25.9 248.6 %all-to-all-start = ((bf16[64,8,27,256]{3,1,2,0:T(8,128)(2,1)}), bf16[64,8,27,256]{3,1,2,0:T(8,128)(2,1)}, u32[]{:S(2)}, u32[]{:S(2)}) async-start(bf16[64,8,27,256]{3,1,2,0:T(8,128)(2,1)} %stack.2), calls=%async_computation | async-start | bytes 14155776 | tf_op jit(solution)/shard_map/all_to_all | solution.py:64
  35.1 769.0 %reduce-scatter.2.cloned.1.call-start = ((), (), s32[]{:S(2)}) async-start(), calls=%async_computation.4 | async-start | bytes 17039360 | tf_op jit(solution)/shard_map/reduce_scatter | solution.py:104
  278.3 8.9 %copy-start = (bf16[64,8,27,256]{3,1,0,2:T(8,128)(2,1)}, bf16[64,8,27,256]{3,1,0,2:T(8,128)(2,1)S(1)}, u32[]{:S(2)}) copy-start(bf16[64,8,27,256]{3,1,0,2:T(8,128)(2,1)S(1)} %copy.18) | copy-start | bytes 21233668
  384.9 3.2 copy-start.1
  806.0 62.3 %all-to-all-start.1 = ((bf16[4,8,27,256]{3,1,2,0:T(8,128)(2,1)}), bf16[4,8,27,256]{3,1,2,0:T(8,128)(2,1)}, u32[]{:S(2)}, u32[]{:S(2)}) async-start(bf16[4,8,27,256]{3,1,2,0:T(8,128)(2,1)} %broadcast_in_dim.15), calls=%async_computation.2 | async-start | bytes 884736 | tf_op jit(solution)/shard_map/all_to_all | solution.py:24
Sparse Core Ops, SparseCore 0:
  9.7 375.1 all-gather.1
  387.4 416.7 reduce-scatter.1
